TPU v7x, 32 devices: a whole 2x2x4 slice. The times are simulated.
32 devices in a mesh: gx: 4 (over z), gy: 4 (over y, x), gz: 2 (over core).
Axes of the slice: x: 2, y: 2, z: 4, core: 2. Of those that a mesh axis runs over, the one named last changes fastest.
Arguments:
- east_wind: float32 [96, 512, 512], P('gz', 'gx', 'gy'), may hold values from -6 to 6
- north_wind: float32 [96, 512, 512], P('gz', 'gx', 'gy'), may hold values from -6 to 6
- vertical_wind: float32 [96, 512, 512], P('gz', 'gx', 'gy'), may hold values from -6 to 6
- geopotential: float32 [96, 512, 512], P('gz', 'gx', 'gy'), may hold values from -6 to 6
- pressure: float32 [96, 512, 512], P('gz', 'gx', 'gy'), may hold values from -6 to 6
- column_mass: float32 [512, 512], P('gx', 'gy'), may hold values from 0.5 to 2
Outputs:
- east_after: float32 [96, 512, 512], P('gz', 'gx', 'gy')
- north_after: float32 [96, 512, 512], P('gz', 'gx', 'gy')
- vertical_after: float32 [96, 512, 512], P('gz', 'gx', 'gy')
- geo_after: float32 [96, 512, 512], P('gz', 'gx', 'gy')
- pressure_after: float32 [96, 512, 512], P('gz', 'gx', 'gy')
All inputs are finite; a program needn't handle non-finite values.
Results may differ from a plain program's by a relative error of at most 0.0003.
Values sent between devices are 32-bit elements; how exact they have to be, the bound alone decides.
A program may use at most 128 MiB of HBM per device.

v0:
```python
import functools

import jax
import jax.numpy as jnp
from jax import lax
from jax.experimental import pallas as pl
from jax.experimental.pallas import tpu as pltpu
from jax.sharding import PartitionSpec as P

ITERS = 3
STIFF = 30.0
PAD = 8
ROWS = 16
PARTS = 2
UNROLL = 24


def roll(value, shift):
    if isinstance(shift, int):
        shift = shift % value.shape[1]
    return pltpu.roll(value, shift, 1)


def kernel(n, ni, nj, sizes, east_in, north_in, vert_in, geo_in, press_in, mass,
           east, north, vert, geo, press,
           pp, up, psum, dvg, mu_s, c_s, planes, bounds,
           row_out, row_in, col_out, col_in, z_out, z_in,
           load_sem, row_send, row_recv, col_send, col_recv, z_send, z_recv):
    nx, ny, nz = sizes
    unroll = max(u for u in range(2, UNROLL + 1) if n % u == 0 and u % 2 == 0)
    ix, iy, iz = lax.axis_index("gx"), lax.axis_index("gy"), lax.axis_index("gz")
    xs = (lax.rem(ix + nx - 1, nx), lax.rem(ix + 1, nx))
    ys = (lax.rem(iy + ny - 1, ny), lax.rem(iy + 1, ny))

    loads = [
        pltpu.make_async_copy(press_in, pp.at[:, pl.ds(PAD, ni), :], load_sem.at[0]),
        pltpu.make_async_copy(east_in, up.at[:, pl.ds(PAD, ni), :], load_sem.at[1]),
        pltpu.make_async_copy(north_in, north, load_sem.at[2]),
        pltpu.make_async_copy(vert_in, vert, load_sem.at[3]),
        pltpu.make_async_copy(geo_in, geo, load_sem.at[4]),
    ]
    for load in loads:
        load.start()

    barrier = pltpu.get_barrier_semaphore()
    for t in range(2):
        pl.semaphore_signal(barrier, inc=1, device_id={"gx": xs[t]})
        pl.semaphore_signal(barrier, inc=1, device_id={"gy": ys[t]})
    for d in range(1, nz):
        pl.semaphore_signal(barrier, inc=1, device_id={"gz": lax.rem(iz + d, nz)})
    pl.semaphore_wait(barrier, 4 + nz - 1)

    def row_copy(slot, t):
        return pltpu.make_async_remote_copy(
            src_ref=row_out.at[slot, t], dst_ref=row_in.at[slot, 1 - t],
            send_sem=row_send.at[slot, t], recv_sem=row_recv.at[slot, 1 - t],
            device_id={"gx": xs[t]})

    span = ni // PARTS

    def part_rows(h):
        return pl.ds(pl.multiple_of(h * span, span), span)

    def col_copy(slot, t, h):
        return pltpu.make_async_remote_copy(
            src_ref=col_out.at[slot, t, part_rows(h), :], dst_ref=col_in.at[slot, 1 - t, part_rows(h), :],
            send_sem=col_send.at[slot, t, h], recv_sem=col_recv.at[slot, 1 - t, h],
            device_id={"gy": ys[t]})

    def z_copy(slot, d, h):
        return pltpu.make_async_remote_copy(
            src_ref=z_out.at[slot, :, part_rows(h), :], dst_ref=z_in.at[slot, d - 1, :, part_rows(h), :],
            send_sem=z_send.at[slot, d - 1, h], recv_sem=z_recv.at[slot, d - 1, h],
            device_id={"gz": lax.rem(iz + d, nz)})

    lane = lax.broadcasted_iota(jnp.int32, (ROWS, nj), 1)
    pair = lane // 2

    def merged(left, right, width):
        left, right = roll(left, width), roll(right, nj - width)
        even = pair % 2 == 0
        return jnp.where(even, right, left), jnp.where(even, left, right)

    def send_rows(slot, ref):
        row_out[slot, 0] = ref[:, PAD : PAD + 2, :]
        row_out[slot, 1] = ref[:, PAD + ni - 2 : PAD + ni, :]
        for t in range(2):
            row_copy(slot, t).start()

    def recv_rows(slot, ref):
        for t in range(2):
            row_copy(slot, t).wait()
        ref[:, PAD - 2 : PAD, :] = row_in[slot, 0]
        ref[:, PAD + ni : PAD + ni + 2, :] = row_in[slot, 1]

    def packed(value, k, packs):
        turned = roll(value, 2 * k + 2)
        return (jnp.where(pair == k + 1, turned, packs[0]), jnp.where(pair == k, turned, packs[1]))

    def strips(body, h=None):
        count = (ni if h is None else span) // ROWS
        first = 0 if h is None else h * count

        @pl.loop(0, count)
        def _(s):
            body(pl.multiple_of((first + s) * ROWS, ROWS))

    def send_cols(slot, load_level):
        def body(r0):
            zero = jnp.zeros((ROWS, nj), jnp.float32)

            def group(q, packs):
                for e in range(unroll):
                    k = q * unroll + e
                    packs = packed(load_level(k, r0), k, packs)
                return packs

            packs = lax.fori_loop(0, n // unroll, group, (zero, zero))
            for t in range(2):
                col_out[slot, t, pl.ds(r0, ROWS), :] = packs[t]

        strips(body)
        for h in range(PARTS):
            for t in range(2):
                col_copy(slot, t, h).start()

    loads[0].wait()
    send_rows(0, pp)
    send_cols(0, lambda k, r0: pp[k, pl.ds(PAD + r0, ROWS), :])
    loads[1].wait()
    send_rows(ITERS, up)
    loads[2].wait()
    send_cols(ITERS, lambda k, r0: north[k, pl.ds(r0, ROWS), :])

    stiff = STIFF * mass[...]
    root = jnp.sqrt(1.0 + 4.0 * stiff)
    major = 0.5 * (1.0 + 2.0 * stiff + root)
    mu_s[...] = stiff / major
    c_s[...] = 1.0 / major
    planes[0] = jnp.log(stiff / major)
    planes[1] = major / root
    planes[2] = major / stiff

    recv_rows(0, pp)
    recv_rows(ITERS, up)
    for slot in (0, ITERS):
        for t in range(2):
            for h in range(PARTS):
                col_copy(slot, t, h).wait()
    loads[3].wait()
    loads[4].wait()

    def pass_one(it, h):
        def body(r0):
            rows = pl.ds(r0, ROWS)
            m, mu, c = mass[rows, :], mu_s[rows, :], c_s[rows, :]
            weak, strong = 0.05 * m, 0.2 * m
            left, right = col_in[it, 0, rows, :], col_in[it, 1, rows, :]
            ends = merged(left, right, 2)
            if it == 0:
                vends = merged(col_in[ITERS, 0, rows, :], col_in[ITERS, 1, rows, :], 1)

            def star(k, parity):
                end = roll(ends[parity], nj - 2 - 2 * k)
                at = pl.ds(PAD + r0, ROWS)
                p = pp[k, at, :]
                low = jnp.where(lane < 2, end, roll(p, 2))
                high = jnp.where(lane >= nj - 2, end, roll(p, nj - 2))
                total = (pp[k, pl.ds(PAD + r0 + 2, ROWS), :] + pp[k, pl.ds(PAD + r0 - 2, ROWS), :]) + (low + high) - 4.0 * p
                if it == 0:
                    v = north[k, rows, :]
                    vend = roll(vends[parity], nj - 2 - 2 * k)
                    vlow = jnp.where(lane < 1, vend, roll(v, 1))
                    vhigh = jnp.where(lane >= nj - 1, vend, roll(v, nj - 1))
                    d = strong * (up[k, pl.ds(PAD + r0 + 1, ROWS), :] - up[k, pl.ds(PAD + r0 - 1, ROWS), :] + (vhigh - vlow))
                    psum[k, at, :] = p
                else:
                    d = dvg[k, rows, :]
                    psum[k, at, :] = psum[k, at, :] + p
                d = d - weak * total
                if it < ITERS - 1:
                    dvg[k, rows, :] = d
                ps = p - d
                press[k, rows, :] = ps
                return ps

            def sweep(k, above, below, state):
                y, dn, weight = state
                f = c * (vert[k, rows, :] + 0.5 * geo[k, rows, :] - (above - below))
                y = mu * y + f
                vert[k, rows, :] = y
                return y, dn + weight * f, weight * mu

            def steps(ks, carry):
                older, newer, state = carry
                for e, k in enumerate(ks):
                    ps = star(k, e % 2)
                    if not (isinstance(k, int) and k == 0):
                        state = sweep(k - 1, ps, older, state)
                    older, newer = newer, ps
                return older, newer, state

            zero = jnp.zeros((ROWS, nj), jnp.float32)
            carry = (zero, zero, (zero, zero, zero + 1.0))
            carry = steps(range(unroll), carry)
            planes_lo = press[0, rows, :]

            def group(q, carry):
                return steps([q * unroll + e for e in range(unroll)], carry)

            older, newer, state = lax.fori_loop(1, n // unroll, group, carry)
            y, dn, _ = sweep(n - 1, zero, older, state)
            z_out[it, 0, rows, :] = y
            z_out[it, 1, rows, :] = dn
            z_out[it, 2, rows, :] = c * planes_lo
            z_out[it, 3, rows, :] = c * newer

        strips(body, h)

    def interface(it, h):
        def body(r0):
            rows = pl.ds(r0, ROWS)
            mu, logmu, kappa, inv = mu_s[rows, :], planes[0, rows, :], planes[1, rows, :], planes[2, rows, :]
            zero = jnp.zeros((ROWS, nj), jnp.float32)

            def power(m):
                if not isinstance(m, int):
                    m = jnp.maximum(m, 0).astype(jnp.float32)
                return jnp.exp(m * logmu)

            near = power(n - 1)
            below, above, to_low, to_high = zero, zero, zero, zero
            pieces = {}

            def piece(d, which):
                if abs(d) >= nz:
                    return zero
                if d == 0:
                    return z_out[it, which, rows, :]
                value = z_in[it, (nz - d - 1) % nz if d > 0 else -d - 1, which, rows, :]
                inside = jnp.logical_and(iz + d >= 0, iz + d < nz)
                return jnp.where(inside, value, 0.0)

            own_up = own_dn = zero
            for d in range(-(nz - 1), nz):
                j = iz + d
                inside = jnp.logical_and(j >= 0, j < nz)
                under, over = piece(d - 1, 3), piece(d + 1, 2)
                upt = piece(d, 0) + near * under - over
                dnt = piece(d, 1) + under - near * over
                if d == 0:
                    own_up, own_dn = upt, dnt
                    delta_low, delta_high = under, over
                elif d < 0:
                    below = below + jnp.where(inside, power(n * (-1 - d)) * upt, 0.0)
                else:
                    above = above + jnp.where(inside, power(n * (d - 1)) * dnt, 0.0)
                to_low = to_low + jnp.where(inside, power(n * j + 1) * dnt, 0.0)
                to_high = to_high + jnp.where(inside, power(n * (nz - 1 - j) + 1) * upt, 0.0)
            q = power(n * nz + 1)
            scale = kappa / (1.0 - q * q)
            alpha = kappa * below + (q * to_high - to_low) * scale * power(n * iz)
            beta = kappa * above + (q * to_low - to_high) * scale * power(n * (nz - 1 - iz))
            far = power(n + 1)
            bounds[2, rows, :] = kappa * mu * own_dn + alpha + beta * far
            bounds[3, rows, :] = kappa * mu * own_up + beta + alpha * far
            alpha = alpha + kappa * delta_low * inv
            beta = beta - kappa * delta_high * inv
            bounds[0, rows, :] = kappa * mu * z_out[it, 0, rows, :] + beta
            bounds[1, rows, :] = alpha * power(n)

        strips(body, h)

    def pass_two(it, h):
        last = it == ITERS - 1

        def body(r0):
            rows = pl.ds(r0, ROWS)
            mu, inv = mu_s[rows, :], planes[2, rows, :]
            half = 0.5 * mass[rows, :]
            zero = jnp.zeros((ROWS, nj), jnp.float32)

            def finish(k, above, below, packs):
                p = press[k, rows, :] - half * (above - below)
                if last:
                    press[k, rows, :] = p
                    return packs
                pp[k, pl.ds(PAD + r0, ROWS), :] = p
                return packed(p, k, packs)

            def steps(ks, carry):
                x, h, older, newer, packs = carry
                for k in ks:
                    x = mu * x + vert[k, rows, :]
                    v = x + h
                    h = h * inv
                    vert[k, rows, :] = v
                    geo[k, rows, :] = geo[k, rows, :] + 0.5 * v
                    if not (isinstance(k, int) and k == n - 1):
                        packs = finish(k + 1, older, v, packs)
                    older, newer = newer, v
                return x, h, older, newer, packs

            top = bounds[3, rows, :]
            carry = (bounds[0, rows, :], bounds[1, rows, :], zero, top, (zero, zero))
            carry = steps([n - 1 - e for e in range(unroll)], carry)

            def group(q, carry):
                return steps([n - 1 - q * unroll - e for e in range(unroll)], carry)

            _, _, older, newer, packs = lax.fori_loop(1, n // unroll, group, carry)
            packs = finish(0, older, bounds[2, rows, :], packs)
            if not last:
                for t in range(2):
                    col_out[it + 1, t, rows, :] = packs[t]

        strips(body, h)

    def winds():
        def body(r0):
            rows = pl.ds(r0, ROWS)
            left = col_in[0, 0, rows, :]
            right = col_in[0, 1, rows, :]
            for it in range(1, ITERS):
                left = left + col_in[it, 0, rows, :]
                right = right + col_in[it, 1, rows, :]

            ends = merged(left, right, 1)

            def group(q, carry):
                for e in range(unroll):
                    k = q * unroll + e
                    end = roll(ends[e % 2], nj - 2 - 2 * k)
                    at = pl.ds(PAD + r0, ROWS)
                    p = psum[k, at, :]
                    east[k, rows, :] = up[k, at, :] - 0.25 * (
                        psum[k, pl.ds(PAD + r0 + 1, ROWS), :] - psum[k, pl.ds(PAD + r0 - 1, ROWS), :])
                    low = jnp.where(lane < 1, end, roll(p, 1))
                    high = jnp.where(lane >= nj - 1, end, roll(p, nj - 1))
                    north[k, rows, :] = north[k, rows, :] - 0.25 * (high - low)
                return carry

            lax.fori_loop(0, n // unroll, group, 0)

        strips(body)

    for it in range(ITERS):
        if it > 0:
            recv_rows(it, pp)

        @pl.loop(0, PARTS)
        def _(h, it=it):
            if it > 0:
                for t in range(2):
                    col_copy(it, t, h).wait()
            pass_one(it, h)
            for d in range(1, nz):
                z_copy(it, d, h).start()

        if it == ITERS - 1:
            for t, at in ((0, PAD - 2), (1, PAD + ni)):
                total = row_in[0, t]
                for slot in range(1, ITERS):
                    total = total + row_in[slot, t]
                psum[:, at : at + 2, :] = total
            winds()

        @pl.loop(0, PARTS)
        def _(h, it=it):
            for d in range(1, nz):
                z_copy(it, d, h).wait()
            interface(it, h)
            pass_two(it, h)
            if it < ITERS - 1:
                for t in range(2):
                    col_copy(it + 1, t, h).start()

        if it < ITERS - 1:
            send_rows(it + 1, pp)


def local(sizes, east, north, vert, geo, press, mass):
    n, ni, nj = east.shape
    nz = sizes[2]
    f32 = jnp.float32
    slots = ITERS + 1
    field = pltpu.VMEM((n, ni, nj), f32)
    padded = pltpu.VMEM((n, ni + 2 * PAD, nj), f32)
    plane = pltpu.VMEM((ni, nj), f32)
    return pl.pallas_call(
        functools.partial(kernel, n, ni, nj, sizes),
        out_shape=[pltpu.VMEM((n, ni, nj), f32)] * 5,
        in_specs=[pl.BlockSpec(memory_space=pl.ANY)] * 5 + [pl.BlockSpec(memory_space=pltpu.VMEM)],
        out_specs=[pl.BlockSpec(memory_space=pltpu.VMEM)] * 5,
        scratch_shapes=[
            padded, padded, padded, field, plane, plane,
            pltpu.VMEM((3, ni, nj), f32),
            pltpu.VMEM((4, ni, nj), f32),
            pltpu.VMEM((slots, 2, n, 2, nj), f32),
            pltpu.VMEM((slots, 2, n, 2, nj), f32),
            pltpu.VMEM((slots, 2, ni, nj), f32),
            pltpu.VMEM((slots, 2, ni, nj), f32),
            pltpu.VMEM((ITERS, 4, ni, nj), f32),
            pltpu.VMEM((ITERS, nz - 1, 4, ni, nj), f32),
            pltpu.SemaphoreType.DMA((5,)),
            pltpu.SemaphoreType.DMA((slots, 2)),
            pltpu.SemaphoreType.DMA((slots, 2)),
            pltpu.SemaphoreType.DMA((slots, 2, PARTS)),
            pltpu.SemaphoreType.DMA((slots, 2, PARTS)),
            pltpu.SemaphoreType.DMA((ITERS, nz - 1, PARTS)),
            pltpu.SemaphoreType.DMA((ITERS, nz - 1, PARTS)),
        ],
        compiler_params=pltpu.CompilerParams(
            collective_id=0, has_side_effects=True, vmem_limit_bytes=40 * 1024 * 1024),
    )(east, north, vert, geo, press, mass)


FRONT = 3


def paired(n, ni, nj, sizes, east_in, north_in, vert_in, geo_in, press_in, mass_in,
           rhs, star, geo, coef, p0, up, north, edge, faces,
           p1, p2, dvg, head, side, mass, con, pack,
           row_out, row_in, col_out, col_in, z_out, z_in,
           load_sem, row_send, row_recv, col_send, col_recv, z_send, z_recv):
    nx, ny, _ = sizes
    per = nj // 4
    count = ni // ROWS
    press = (p0, p1, p2)
    ix, iy, iz = lax.axis_index("gx"), lax.axis_index("gy"), lax.axis_index("gz")
    xs = (lax.rem(ix + nx - 1, nx), lax.rem(ix + 1, nx))
    ys = (lax.rem(iy + ny - 1, ny), lax.rem(iy + 1, ny))
    flip = (1 - 2 * iz).astype(jnp.float32)
    inner = pl.ds(PAD, ni)

    fields = (
        (press_in, p0.at[:, inner, :]), (north_in, north), (east_in, up.at[:, inner, :]),
        (vert_in, head), (geo_in, geo))
    mass_load = pltpu.make_async_copy(mass_in, mass, load_sem.at[5])
    mass_load.start()
    for e, (src, dst) in enumerate(fields):
        @pl.loop(0, n)
        def _(m, e=e, src=src, dst=dst):
            k = iz * (n - 1) + (1 - 2 * iz) * m
            pltpu.make_async_copy(src.at[k], dst.at[m], load_sem.at[e]).start()

    def loaded(e):
        pltpu.make_async_copy(fields[e][0], fields[e][1], load_sem.at[e]).wait()

    barrier = pltpu.get_barrier_semaphore()
    for t in range(2):
        pl.semaphore_signal(barrier, inc=1, device_id={"gx": xs[t]})
        pl.semaphore_signal(barrier, inc=1, device_id={"gy": ys[t]})
    pl.semaphore_signal(barrier, inc=1, device_id={"gz": 1 - iz})

    def row_copy(it, t):
        return pltpu.make_async_remote_copy(
            src_ref=row_out.at[it, t], dst_ref=row_in.at[it, 1 - t],
            send_sem=row_send.at[it, t], recv_sem=row_recv.at[it, 1 - t],
            device_id={"gx": xs[t]})

    def rows_of(s):
        return pl.ds(pl.multiple_of(s * ROWS, ROWS), ROWS)

    def col_copy(it, t, s):
        return pltpu.make_async_remote_copy(
            src_ref=col_out.at[it, t, rows_of(s), :], dst_ref=col_in.at[it, 1 - t, rows_of(s), :],
            send_sem=col_send.at[it, t, s], recv_sem=col_recv.at[it, 1 - t, s],
            device_id={"gy": ys[t]})

    def z_copy(it, s):
        return pltpu.make_async_remote_copy(
            src_ref=z_out.at[it, :, rows_of(s), :], dst_ref=z_in.at[it, :, rows_of(s), :],
            send_sem=z_send.at[it, s], recv_sem=z_recv.at[it, s],
            device_id={"gz": 1 - iz})

    lane = lax.broadcasted_iota(jnp.int32, (ROWS, nj), 1)
    quad, part = lane // 4, lane % 4
    zero = jnp.zeros((ROWS, nj), jnp.float32)

    def packed(value, m, packs):
        turned = roll(value, 4 * (m % per) + 2)
        b = m // per
        return tuple(jnp.where(quad == m % per, turned, packs[c]) if c == b else packs[c] for c in range(2))

    def outgoing(it, rows, packs):
        a, b = packs
        col_out[it, 0, rows, :] = jnp.where(part >= 2, a, roll(b, -2))
        col_out[it, 1, rows, :] = jnp.where(part < 2, a, roll(b, 2))

    def incoming(left, right):
        return (jnp.where(part < 2, roll(right, -2), roll(left, 2)),
                jnp.where(part < 2, right, left))

    def sides(value, ends, m, width):
        end = roll(ends[m // per], nj - 2 - 4 * (m % per))
        low = jnp.where(lane < width, end, roll(value, width))
        high = jnp.where(lane >= nj - width, end, roll(value, nj - width))
        return low, high

    loaded(0)
    loaded(1)

    @pl.loop(0, count)
    def _(s):
        rows = rows_of(s)
        at = pl.ds(PAD + pl.multiple_of(s * ROWS, ROWS), ROWS)
        pk, vk = (zero, zero), (zero, zero)
        for m in range(n):
            pk = packed(p0[m, at, :], m, pk)
            vk = packed(north[m, rows, :], m, vk)
        packs = tuple(
            a + jnp.where(part == 0, 4.0 * roll(v, -1), jnp.where(part == 3, -4.0 * roll(v, 1), 0.0))
            for a, v in zip(pk, vk))
        outgoing(0, rows, packs)

    loaded(2)
    up[:, :PAD, :] = jnp.zeros((n, PAD, nj), jnp.float32)
    up[:, PAD + ni :, :] = jnp.zeros((n, PAD, nj), jnp.float32)
    row_out[0, 0] = p0[:, PAD : PAD + 2, :] - 4.0 * up[:, PAD - 1 : PAD + 1, :]
    row_out[0, 1] = p0[:, PAD + ni - 2 : PAD + ni, :] + 4.0 * up[:, PAD + ni - 1 : PAD + ni + 1, :]

    pl.semaphore_wait(barrier, 5)

    @pl.loop(0, count)
    def _(s):
        for t in range(2):
            col_copy(0, t, s).start()

    for t in range(2):
        row_copy(0, t).start()

    mass_load.wait()
    inverse = 1.0 / (STIFF * mass[...])
    con[0] = 1.25 * inverse
    con[1] = 0.25 * inverse
    base = 2.0 + inverse

    def pivot(m, a):
        a = 1.0 / (base - a)
        coef[m] = a
        return a

    last = lax.fori_loop(0, n, pivot, jnp.zeros((ni, nj), jnp.float32))
    con[2] = last / (1.0 - last * last)

    @pl.loop(0, count)
    def _(s):
        rows = rows_of(s)
        r0 = PAD + pl.multiple_of(s * ROWS, ROWS)
        strong = 0.2 * mass[rows, :]
        for m in range(n):
            v = north[m, rows, :]
            low = jnp.where(lane < 1, 0.0, roll(v, 1))
            high = jnp.where(lane >= nj - 1, 0.0, roll(v, nj - 1))
            dvg[m, rows, :] = strong * (
                (up[m, pl.ds(r0 + 1, ROWS), :] - up[m, pl.ds(r0 - 1, ROWS), :]) + (high - low))

    loaded(3)
    loaded(4)

    @pl.loop(0, count)
    def _(s):
        rows = rows_of(s)
        for m in range(n):
            g = (0.5 * flip) * geo[m, rows, :]
            geo[m, rows, :] = g
            head[m, rows, :] = flip * head[m, rows, :] + g

    def lateral(it, s):
        rows = rows_of(s)
        at = pl.ds(PAD + pl.multiple_of(s * ROWS, ROWS), ROWS)
        ends = incoming(col_in[it, 0, rows, :], col_in[it, 1, rows, :])

        def level(m):
            low, high = sides(press[it][m, at, :], ends, m, 2)
            side[m] = low + high

        return level

    def forward(it, s):
        rows = rows_of(s)
        r0 = PAD + pl.multiple_of(s * ROWS, ROWS)
        at = pl.ds(r0, ROWS)
        weak = 0.05 * mass[rows, :]
        four = 4.0 * weak
        state = {"older": zero, "newer": None, "g": None}

        def close(m, above):
            g = head[m, rows, :] - (above - state["older"])
            if m > 0:
                g = g + coef[m - 1, rows, :] * state["g"]
            rhs[m, rows, :] = g
            state["g"] = g

        def level(m):
            ref = press[it]
            p = ref[m, at, :]
            total = (ref[m, pl.ds(r0 + 2, ROWS), :] + ref[m, pl.ds(r0 - 2, ROWS), :]) + side[m]
            d = (dvg[m, rows, :] + four * p) - weak * total
            if it < ITERS - 1:
                dvg[m, rows, :] = d
            else:
                p0[m, at, :] = (p0[m, at, :] + p1[m, at, :]) + p
            ps = p - d
            star[m, rows, :] = ps
            if m > 0:
                close(m - 1, ps)
                state["older"] = state["newer"]
            state["newer"] = ps

        def finish():
            close(n - 1, zero)
            z_out[it, 0, rows, :] = state["g"]
            z_out[it, 1, rows, :] = state["newer"]
            z_copy(it, s).start()

        return level, finish

    def col_wait(it, s):
        for t in range(2):
            col_copy(it, t, s).wait()

    def row_wait(it):
        for t in range(2):
            row_copy(it, t).wait()
        press[it][:, PAD - 2 : PAD, :] = row_in[it, 0]
        press[it][:, PAD + ni : PAD + ni + 2, :] = row_in[it, 1]

    def pass_one(it):
        col_wait(it, 1)
        level = lateral(it, 1)
        for m in range(n):
            level(m)

        @pl.loop(1, count)
        def _(s):
            @pl.when(s == count - 1)
            def _():
                row_wait(it)

            after = lax.rem(s + 1, count)
            col_wait(it, after)
            level, finish = forward(it, s)
            ahead = lateral(it, after)
            for m in range(n):
                level(m)
                ahead(m)
            finish()

        level, finish = forward(it, 0)
        for m in range(n):
            level(m)
        finish()

    def interface(it, s):
        rows = rows_of(s)
        z_copy(it, s).wait()
        a, w = coef[n - 1, rows, :], con[2, rows, :]
        mine = z_out[it, 0, rows, :] - z_in[it, 1, rows, :]
        other = z_in[it, 0, rows, :] - z_out[it, 1, rows, :]
        z = w * (mine - a * other)
        return z, a * (z - other)

    def backward(it, s):
        rows = rows_of(s)
        at = pl.ds(PAD + pl.multiple_of(s * ROWS, ROWS), ROWS)
        near, far = con[0, rows, :], con[1, rows, :]
        z, above = interface(it, s)
        packs = (zero, zero)
        for m in range(n - 1, -1, -1):
            g = geo[m, rows, :]
            head[m, rows, :] = near * z + g
            geo[m, rows, :] = far * z + g
            below = coef[m - 1, rows, :] * (rhs[m - 1, rows, :] + z) if m > 0 else zero
            p = star[m, rows, :] - (0.5 / STIFF) * (above - below)
            press[it + 1][m, at, :] = p
            packs = packed(p, m, packs)
            above, z = z, below
        outgoing(it + 1, rows, packs)
        for t in range(2):
            col_copy(it + 1, t, s).start()

    def pass_two(it):
        @pl.loop(0, count)
        def _(t):
            s = jnp.where(t < FRONT, t + 1, jnp.where(t == FRONT, count - 1, jnp.where(t == FRONT + 1, 0, t - 1)))
            backward(it, s)

            @pl.when(t == FRONT)
            def _():
                row_out[it + 1, 1] = press[it + 1][:, PAD + ni - 2 : PAD + ni, :]
                row_copy(it + 1, 1).start()

            @pl.when(t == FRONT + 1)
            def _():
                row_out[it + 1, 0] = press[it + 1][:, PAD : PAD + 2, :]
                row_copy(it + 1, 0).start()

    for it in range(ITERS):
        pass_one(it)
        if it < ITERS - 1:
            pass_two(it)

    for t, at in ((0, PAD - 2), (1, PAD + ni)):
        p0[:, at : at + 2, :] = (row_in[0, t] + row_in[1, t]) + row_in[2, t]

    def closing(s):
        rows = rows_of(s)
        left = (col_in[0, 0, rows, :] + col_in[1, 0, rows, :]) + col_in[2, 0, rows, :]
        right = (col_in[0, 1, rows, :] + col_in[1, 1, rows, :]) + col_in[2, 1, rows, :]
        edge[0, rows, :] = jnp.where(part == 1, roll(right, -1), roll(left, 1))
        edge[1, rows, :] = jnp.where(part == 1, roll(right, 1), roll(left, -1))

    @pl.loop(0, count)
    def _(s):
        closing(s)

    @pl.loop(0, count)
    def _(t):
        s = lax.rem(t + 1, count)
        faces[0, rows_of(s), :], faces[1, rows_of(s), :] = interface(ITERS - 1, s)


def finale(n, ni, nj, rhs, star, geo, coef, psum, up, north, edge, faces, mass,
           east_out, north_out, vert_out, geo_out, press_out,
           east_s, north_s, vert_s, geo_s, press_s, sem):
    per = nj // 4
    count = ni // ROWS
    iz = lax.axis_index("gz")
    flip = (1 - 2 * iz).astype(jnp.float32)
    lane = lax.broadcasted_iota(jnp.int32, (ROWS, nj), 1)

    def store(e, src, dst, rows):
        return pltpu.make_async_copy(src.at[:, rows, :], dst.at[:, rows, :], sem.at[e])

    outs = ((east_s, east_out), (north_s, north_out), (vert_s, vert_out), (geo_s, geo_out), (press_s, press_out))

    def level_of(m):
        return iz * (n - 1) + (1 - 2 * iz) * m

    @pl.loop(0, count)
    def _(s):
        rows = pl.ds(pl.multiple_of(s * ROWS, ROWS), ROWS)
        v_of = flip / (STIFF * mass[rows, :])
        half = 0.5 * v_of
        twice = 2.0 * flip
        z, above = faces[0, rows, :], faces[1, rows, :]
        for m in range(n - 1, -1, -1):
            k = level_of(m)
            vert_s[k, rows, :] = v_of * z
            geo_s[k, rows, :] = twice * geo[m, rows, :] + half * z
            below = coef[m - 1, rows, :] * (rhs[m - 1, rows, :] + z) if m > 0 else jnp.zeros_like(z)
            press_s[k, rows, :] = star[m, rows, :] - (0.5 / STIFF) * (above - below)
            above, z = z, below
        for e in (2, 3, 4):
            store(e, *outs[e], rows).start()

    @pl.loop(0, count)
    def _(s):
        rows = pl.ds(pl.multiple_of(s * ROWS, ROWS), ROWS)
        r0 = PAD + pl.multiple_of(s * ROWS, ROWS)
        ends = (edge[0, rows, :], edge[1, rows, :])
        for m in range(n):
            k = level_of(m)
            p = psum[m, pl.ds(r0, ROWS), :]
            end = roll(ends[m // per], nj - 2 - 4 * (m % per))
            low = jnp.where(lane < 1, end, roll(p, 1))
            high = jnp.where(lane >= nj - 1, end, roll(p, nj - 1))
            north_s[k, rows, :] = north[m, rows, :] - 0.25 * (high - low)
            east_s[k, rows, :] = up[m, pl.ds(r0, ROWS), :] - 0.25 * (
                psum[m, pl.ds(r0 + 1, ROWS), :] - psum[m, pl.ds(r0 - 1, ROWS), :])
        for e in (0, 1):
            store(e, *outs[e], rows).start()

    for e in range(5):
        pltpu.make_async_copy(outs[e][0], outs[e][1], sem.at[e]).wait()


def pair(sizes, east, north, vert, geo, press, mass):
    n, ni, nj = east.shape
    f32 = jnp.float32
    count = ni // ROWS
    shape = (n, ni, nj)
    padded = (n, ni + 2 * PAD, nj)
    kept = [shape, shape, shape, shape, padded, padded, shape, (2, ni, nj), (2, ni, nj)]
    vmem = pl.BlockSpec(memory_space=pltpu.VMEM)
    state = pl.pallas_call(
        functools.partial(paired, n, ni, nj, sizes),
        out_shape=[pltpu.VMEM(s, f32) for s in kept],
        in_specs=[pl.BlockSpec(memory_space=pl.ANY)] * 6,
        out_specs=[vmem] * len(kept),
        scratch_shapes=[
            pltpu.VMEM(padded, f32), pltpu.VMEM(padded, f32), pltpu.VMEM(shape, f32), pltpu.VMEM(shape, f32),
            pltpu.VMEM((n, ROWS, nj), f32),
            pltpu.VMEM((ni, nj), f32),
            pltpu.VMEM((3, ni, nj), f32),
            pltpu.VMEM((2, ni, nj), f32),
            pltpu.VMEM((ITERS, 2, n, 2, nj), f32),
            pltpu.VMEM((ITERS, 2, n, 2, nj), f32),
            pltpu.VMEM((ITERS, 2, ni, nj), f32),
            pltpu.VMEM((ITERS, 2, ni, nj), f32),
            pltpu.VMEM((ITERS, 2, ni, nj), f32),
            pltpu.VMEM((ITERS, 2, ni, nj), f32),
            pltpu.SemaphoreType.DMA((6,)),
            pltpu.SemaphoreType.DMA((ITERS, 2)),
            pltpu.SemaphoreType.DMA((ITERS, 2)),
            pltpu.SemaphoreType.DMA((ITERS, 2, count)),
            pltpu.SemaphoreType.DMA((ITERS, 2, count)),
            pltpu.SemaphoreType.DMA((ITERS, count)),
            pltpu.SemaphoreType.DMA((ITERS, count)),
        ],
        compiler_params=pltpu.CompilerParams(
            collective_id=0, has_side_effects=True, vmem_limit_bytes=25 * 1024 * 1024),
    )(east, north, vert, geo, press, mass)
    return pl.pallas_call(
        functools.partial(finale, n, ni, nj),
        out_shape=[jax.ShapeDtypeStruct(shape, f32)] * 5,
        in_specs=[vmem] * (len(kept) + 1),
        out_specs=[pl.BlockSpec(memory_space=pl.ANY)] * 5,
        scratch_shapes=[pltpu.VMEM(shape, f32)] * 5 + [pltpu.SemaphoreType.DMA((5,))],
        compiler_params=pltpu.CompilerParams(vmem_limit_bytes=18 * 1024 * 1024),
    )(*state, mass)


def solution(mesh):
    sizes = (mesh.shape["gx"], mesh.shape["gy"], mesh.shape["gz"])
    cube = P("gz", "gx", "gy")

    def body(east, *rest):
        n, ni, nj = east.shape
        fits = sizes[2] == 2 and n <= nj // 2 and ni // ROWS > FRONT + 2 and ITERS == 3
        return (pair if fits else local)(sizes, east, *rest)

    return jax.shard_map(
        body, mesh=mesh,
        in_specs=(cube,) * 5 + (P("gx", "gy"),), out_specs=(cube,) * 5, check_vma=False)
```

profile of v0, /device:TPU:0, one launch (start us, length us, event | category | flops | bytes accessed | tf_op | source)
XLA Modules:
  0.0 51.6 jit_solution(15697767280151117716)
XLA Ops:
  0.6 0.0 copy-start
  0.6 1.9 %copy-done = f32[48,128,128]{2,1,0:T(8,128)S(1)} copy-done((f32[48,128,128]{2,1,0:T(8,128)S(1)}, f32[48,128,128]{2,1,0:T(8,128)}, u32[]{:S(2)}) %copy-start) | copy-done | bytes 3145752
  2.5 0.0 copy-start.1
  2.5 1.9 %copy-done.1 = f32[48,128,128]{2,1,0:T(8,128)S(1)} copy-done((f32[48,128,128]{2,1,0:T(8,128)S(1)}, f32[48,128,128]{2,1,0:T(8,128)}, u32[]{:S(2)}) %copy-start.1) | copy-done | bytes 3145752
  4.4 0.0 copy-start.2
  4.4 0.8 %copy-done.2 = f32[128,128]{1,0:T(8,128)S(1)} copy-done((f32[128,128]{1,0:T(8,128)S(1)}, f32[128,128]{1,0:T(8,128)}, u32[]{:S(2)}) %copy-start.2) | copy-done | bytes 65560
  5.3 40.4 %shard_map.101 = (f32[48,128,128]{2,1,0:T(8,128)S(1)}, f32[48,128,128]{2,1,0:T(8,128)S(1)}, f32[48,128,128]{2,1,0:T(8,128)S(1)}, f32[48,128,128]{2,1,0:T(8,128)S...) custom-call(f32[48,128,128]{2,1,0:T(8,128)S(1)} %copy-done, ...), custom_call_target="tpu_custom_call" | custom-call | tf_op jit(solution)/shard_map/pallas_call | solution.py:788
  45.6 5.9 %shard_map.102 = (f32[48,128,128]{2,1,0:T(8,128)}, f32[48,128,128]{2,1,0:T(8,128)}, f32[48,128,128]{2,1,0:T(8,128)}, f32[48,128,128]{2,1,0:T(8,128)}, f32[48,128,128]{2,1,0:T(8,128)}) custom-call(f32[48,128,128]{2,1,0:T(8,128)S(1)} %get-tuple-element.14.rhs, f32[48,128,128]{2,1,0:T(8,128)S(1)} %get-tuple-element.15.star, ...), custom_call_target="tpu_custom_call" | custom-call | tf_op jit(solution)/shard_map/pallas_call | solution.py:816
Async XLA Ops:
  0.6 1.9 %copy-start = (f32[48,128,128]{2,1,0:T(8,128)S(1)}, f32[48,128,128]{2,1,0:T(8,128)}, u32[]{:S(2)}) copy-start(f32[48,128,128]{2,1,0:T(8,128)} %east_in.1) | copy-start | bytes 9437188
  2.5 1.9 %copy-start.1 = (f32[48,128,128]{2,1,0:T(8,128)S(1)}, f32[48,128,128]{2,1,0:T(8,128)}, u32[]{:S(2)}) copy-start(f32[48,128,128]{2,1,0:T(8,128)} %north_in.1) | copy-start | bytes 9437188
  4.4 0.8 %copy-start.2 = (f32[128,128]{1,0:T(8,128)S(1)}, f32[128,128]{1,0:T(8,128)}, u32[]{:S(2)}) copy-start(f32[128,128]{1,0:T(8,128)} %mass.1) | copy-start | bytes 196612
where the time goes:
time: 51.8 us; the launch traced here: 51.6 us
  Pallas kernels  46.3 us (89%)
  local copies, waits for them, and re-layouts  4.61 us (9%)
  between operations  0.65 us (1%)
    pallas_call x1, Pallas kernels, pair(): pl.pallas_call(functools.partial(paired, n, ni, nj, sizes), out_shape=[pl...  40.4 us
    pallas_call x1, Pallas kernels, pair(): pl.pallas_call(functools.partial(finale, n, ni, nj), out_shape=[jax.Shape...  5.94 us
    unnamed x6, local copies, waits for them, and re-layouts  4.61 us

commit v1 on v0

--- a/solution.py
+++ b/solution.py
@@ -416,11 +416,12 @@
 
 
 FRONT = 3
+WIDE = 32
 
 
 def paired(n, ni, nj, sizes, east_in, north_in, vert_in, geo_in, press_in, mass_in,
            rhs, star, geo, coef, p0, up, north, edge, faces,
-           p1, p2, dvg, head, side, mass, con, pack,
+           p1, p2, dvg, head, turned, side, mass, con, packs_p, packs_v,
            row_out, row_in, col_out, col_in, z_out, z_in,
            load_sem, row_send, row_recv, col_send, col_recv, z_send, z_recv):
     nx, ny, _ = sizes
@@ -475,13 +476,12 @@
             device_id={"gz": 1 - iz})
 
     lane = lax.broadcasted_iota(jnp.int32, (ROWS, nj), 1)
-    quad, part = lane // 4, lane % 4
+    part, couple = lane % 4, lane // 2
     zero = jnp.zeros((ROWS, nj), jnp.float32)
 
-    def packed(value, m, packs):
-        turned = roll(value, 4 * (m % per) + 2)
+    def placed(quad, value, m, packs):
         b = m // per
-        return tuple(jnp.where(quad == m % per, turned, packs[c]) if c == b else packs[c] for c in range(2))
+        return tuple(jnp.where(quad == m % per, value, packs[c]) if c == b else packs[c] for c in range(2))
 
     def outgoing(it, rows, packs):
         a, b = packs
@@ -489,44 +489,51 @@
         col_out[it, 1, rows, :] = jnp.where(part < 2, a, roll(b, 2))
 
     def incoming(left, right):
-        return (jnp.where(part < 2, roll(right, -2), roll(left, 2)),
-                jnp.where(part < 2, right, left))
-
-    def sides(value, ends, m, width):
-        end = roll(ends[m // per], nj - 2 - 4 * (m % per))
-        low = jnp.where(lane < width, end, roll(value, width))
-        high = jnp.where(lane >= nj - width, end, roll(value, nj - width))
-        return low, high
+        return (jnp.where(part < 2, left, right),
+                jnp.where(part < 2, roll(left, -2), roll(right, 2)))
+
+    def gather(ref, pad, packs, keep):
+        quad = lax.broadcasted_iota(jnp.int32, (WIDE, nj), 1) // 4
+
+        @pl.loop(0, ni // WIDE)
+        def _(s):
+            r0 = pl.multiple_of(s * WIDE, WIDE)
+            rows = pl.ds(r0, WIDE)
+            got = (jnp.zeros((WIDE, nj), jnp.float32),) * 2
+            for m in range(n):
+                value = roll(ref[m, pl.ds(pad + r0, WIDE), :], 4 * (m % per) + 2)
+                if keep:
+                    turned[m, rows, :] = value
+                got = placed(quad, value, m, got)
+            packs[0, rows, :], packs[1, rows, :] = got
 
     loaded(0)
+    gather(p0, PAD, packs_p, True)
     loaded(1)
+    gather(north, 0, packs_v, False)
 
     @pl.loop(0, count)
     def _(s):
         rows = rows_of(s)
-        at = pl.ds(PAD + pl.multiple_of(s * ROWS, ROWS), ROWS)
-        pk, vk = (zero, zero), (zero, zero)
-        for m in range(n):
-            pk = packed(p0[m, at, :], m, pk)
-            vk = packed(north[m, rows, :], m, vk)
-        packs = tuple(
-            a + jnp.where(part == 0, 4.0 * roll(v, -1), jnp.where(part == 3, -4.0 * roll(v, 1), 0.0))
-            for a, v in zip(pk, vk))
+        packs = []
+        for c in range(2):
+            v = packs_v[c, rows, :]
+            packs.append(packs_p[c, rows, :] + jnp.where(
+                part == 0, 4.0 * roll(v, -1), jnp.where(part == 3, -4.0 * roll(v, 1), 0.0)))
         outgoing(0, rows, packs)
+
+    pl.semaphore_wait(barrier, 5)
+
+    @pl.loop(0, count)
+    def _(s):
+        for t in range(2):
+            col_copy(0, t, s).start()
 
     loaded(2)
     up[:, :PAD, :] = jnp.zeros((n, PAD, nj), jnp.float32)
     up[:, PAD + ni :, :] = jnp.zeros((n, PAD, nj), jnp.float32)
     row_out[0, 0] = p0[:, PAD : PAD + 2, :] - 4.0 * up[:, PAD - 1 : PAD + 1, :]
     row_out[0, 1] = p0[:, PAD + ni - 2 : PAD + ni, :] + 4.0 * up[:, PAD + ni - 1 : PAD + ni + 1, :]
-
-    pl.semaphore_wait(barrier, 5)
-
-    @pl.loop(0, count)
-    def _(s):
-        for t in range(2):
-            col_copy(0, t, s).start()
-
     for t in range(2):
         row_copy(0, t).start()
 
@@ -569,11 +576,13 @@
 
     def lateral(it, s):
         rows = rows_of(s)
-        at = pl.ds(PAD + pl.multiple_of(s * ROWS, ROWS), ROWS)
         ends = incoming(col_in[it, 0, rows, :], col_in[it, 1, rows, :])
 
         def level(m):
-            low, high = sides(press[it][m, at, :], ends, m, 2)
+            q, end = m % per, ends[m // per]
+            value = turned[m, rows, :]
+            low = roll(jnp.where(couple == 2 * q, end, value), -4 * q)
+            high = roll(jnp.where(couple == 2 * q + 1, end, value), -4 * q - 4)
             side[m] = low + high
 
         return level
@@ -666,26 +675,54 @@
         rows = rows_of(s)
         at = pl.ds(PAD + pl.multiple_of(s * ROWS, ROWS), ROWS)
         near, far = con[0, rows, :], con[1, rows, :]
-        z, above = interface(it, s)
-        packs = (zero, zero)
-        for m in range(n - 1, -1, -1):
+        state = dict(zip(("z", "above"), interface(it, s)))
+
+        def level(m):
+            z = state["z"]
             g = geo[m, rows, :]
             head[m, rows, :] = near * z + g
             geo[m, rows, :] = far * z + g
             below = coef[m - 1, rows, :] * (rhs[m - 1, rows, :] + z) if m > 0 else zero
-            p = star[m, rows, :] - (0.5 / STIFF) * (above - below)
-            press[it + 1][m, at, :] = p
-            packs = packed(p, m, packs)
-            above, z = z, below
-        outgoing(it + 1, rows, packs)
-        for t in range(2):
-            col_copy(it + 1, t, s).start()
+            press[it + 1][m, at, :] = star[m, rows, :] - (0.5 / STIFF) * (state["above"] - below)
+            state["above"], state["z"] = z, below
+
+        return level
+
+    def skew(it, s):
+        rows = rows_of(s)
+        at = pl.ds(PAD + pl.multiple_of(s * ROWS, ROWS), ROWS)
+        state = {"packs": (zero, zero)}
+        quad = lane // 4
+
+        def level(m):
+            value = roll(press[it][m, at, :], 4 * (m % per) + 2)
+            turned[m, rows, :] = value
+            state["packs"] = placed(quad, value, m, state["packs"])
+
+        def finish():
+            outgoing(it, rows, state["packs"])
+            for t in range(2):
+                col_copy(it, t, s).start()
+
+        return level, finish
+
+    def order(t):
+        return jnp.where(t < FRONT, t + 1, jnp.where(t == FRONT, count - 1, jnp.where(t == FRONT + 1, 0, t - 1)))
 
     def pass_two(it):
-        @pl.loop(0, count)
+        level = backward(it, 1)
+        for m in range(n - 1, -1, -1):
+            level(m)
+
+        @pl.loop(1, count)
         def _(t):
-            s = jnp.where(t < FRONT, t + 1, jnp.where(t == FRONT, count - 1, jnp.where(t == FRONT + 1, 0, t - 1)))
-            backward(it, s)
+            level = backward(it, order(t))
+            behind, finish = skew(it + 1, order(t - 1))
+            for e in range(n):
+                for m in range(2 * e, min(2 * e + 2, n)):
+                    behind(n - 1 - m)
+                level(n - 1 - e)
+            finish()
 
             @pl.when(t == FRONT)
             def _():
@@ -696,6 +733,11 @@
             def _():
                 row_out[it + 1, 0] = press[it + 1][:, PAD : PAD + 2, :]
                 row_copy(it + 1, 0).start()
+
+        behind, finish = skew(it + 1, count - 2)
+        for m in range(n - 1, -1, -1):
+            behind(m)
+        finish()
 
     for it in range(ITERS):
         pass_one(it)
@@ -788,13 +830,15 @@
     state = pl.pallas_call(
         functools.partial(paired, n, ni, nj, sizes),
         out_shape=[pltpu.VMEM(s, f32) for s in kept],
-        in_specs=[pl.BlockSpec(memory_space=pl.ANY)] * 6,
+        in_specs=[pl.BlockSpec(memory_space=pltpu.HBM)] * 6,
         out_specs=[vmem] * len(kept),
         scratch_shapes=[
             pltpu.VMEM(padded, f32), pltpu.VMEM(padded, f32), pltpu.VMEM(shape, f32), pltpu.VMEM(shape, f32),
+            pltpu.VMEM(shape, f32),
             pltpu.VMEM((n, ROWS, nj), f32),
             pltpu.VMEM((ni, nj), f32),
             pltpu.VMEM((3, ni, nj), f32),
+            pltpu.VMEM((2, ni, nj), f32),
             pltpu.VMEM((2, ni, nj), f32),
             pltpu.VMEM((ITERS, 2, n, 2, nj), f32),
             pltpu.VMEM((ITERS, 2, n, 2, nj), f32),
@@ -811,7 +855,7 @@
             pltpu.SemaphoreType.DMA((ITERS, count)),
         ],
         compiler_params=pltpu.CompilerParams(
-            collective_id=0, has_side_effects=True, vmem_limit_bytes=25 * 1024 * 1024),
+            collective_id=0, has_side_effects=True, vmem_limit_bytes=41 * 1024 * 1024),
     )(east, north, vert, geo, press, mass)
     return pl.pallas_call(
         functools.partial(finale, n, ni, nj),
@@ -829,7 +873,7 @@
 
     def body(east, *rest):
         n, ni, nj = east.shape
-        fits = sizes[2] == 2 and n <= nj // 2 and ni // ROWS > FRONT + 2 and ITERS == 3
+        fits = sizes[2] == 2 and n <= nj // 2 and ni // ROWS > FRONT + 2 and ni % WIDE == 0 and ITERS == 3
         return (pair if fits else local)(sizes, east, *rest)
 
     return jax.shard_map(

time: 51.8 us -> 38.4 us (0.74)
  Pallas kernels: 46.3 us -> 37.5 us
  local copies, waits for them, and re-layouts: 4.61 us -> 0.01 us
    pallas_call x1, Pallas kernels: 40.4 us -> 31.6 us  [pair(): pl.pallas_call(functools.partial(paired, n, ni, nj, sizes), out_shape=[pl...]
    unnamed x6 -> x2, local copies, waits for them, and re-layouts: 4.61 us -> 0.01 us
where the time goes in v1:
time: 38.4 us; the launch traced here: 38.2 us
  Pallas kernels  37.5 us (98%)
  between operations  0.66 us (2%)
    pallas_call x1, Pallas kernels, pair(): pl.pallas_call(functools.partial(paired, n, ni, nj, sizes), out_shape=[pl...  31.6 us
    pallas_call x1, Pallas kernels, pair(): pl.pallas_call(functools.partial(finale, n, ni, nj), out_shape=[jax.Shape...  5.94 us

profile of v1, /device:TPU:0, one launch (start us, length us, event | category | flops | bytes accessed | tf_op | source)
XLA Modules:
  0.0 38.2 jit_solution(2246153291908796486)
XLA Ops:
  0.6 0.0 copy-start
  0.6 31.6 %shard_map.101 = (f32[48,128,128]{2,1,0:T(8,128)S(1)}, f32[48,128,128]{2,1,0:T(8,128)S(1)}, f32[48,128,128]{2,1,0:T(8,128)S(1)}, f32[48,128,128]{2,1,0:T(8,128)S...) custom-call(f32[48,128,128]{2,1,0:T(8,128)} %east_in.1, ...), custom_call_target="tpu_custom_call" | custom-call | tf_op jit(solution)/shard_map/pallas_call | solution.py:830
  32.3 0.0 copy-done
  32.3 5.9 %shard_map.102 = (f32[48,128,128]{2,1,0:T(8,128)}, f32[48,128,128]{2,1,0:T(8,128)}, f32[48,128,128]{2,1,0:T(8,128)}, f32[48,128,128]{2,1,0:T(8,128)}, f32[48,128,128]{2,1,0:T(8,128)}) custom-call(f32[48,128,128]{2,1,0:T(8,128)S(1)} %get-tuple-element.14.rhs, f32[48,128,128]{2,1,0:T(8,128)S(1)} %get-tuple-element.15.star, ...), custom_call_target="tpu_custom_call" | custom-call | tf_op jit(solution)/shard_map/pallas_call | solution.py:860
Async XLA Ops:
  0.6 31.6 %copy-start = (f32[128,128]{1,0:T(8,128)S(1)}, f32[128,128]{1,0:T(8,128)}, u32[]{:S(2)}) copy-start(f32[128,128]{1,0:T(8,128)} %mass.1) | copy-start | bytes 196612

commit v2 on v0

--- a/solution.py
+++ b/solution.py
@@ -415,37 +415,27 @@
     )(east, north, vert, geo, press, mass)
 
 
-FRONT = 3
+LAG = 3
+TILE = 32
+WIDE = 32
 
 
 def paired(n, ni, nj, sizes, east_in, north_in, vert_in, geo_in, press_in, mass_in,
            rhs, star, geo, coef, p0, up, north, edge, faces,
-           p1, p2, dvg, head, side, mass, con, pack,
+           p1, p2, dvg, head, turned_a, turned_b, turned_c, side, mass, con, packs_p, packs_v,
            row_out, row_in, col_out, col_in, z_out, z_in,
            load_sem, row_send, row_recv, col_send, col_recv, z_send, z_recv):
     nx, ny, _ = sizes
     per = nj // 4
-    count = ni // ROWS
+    count = ni // TILE
     press = (p0, p1, p2)
+    turned = (turned_a, turned_c, turned_a)
     ix, iy, iz = lax.axis_index("gx"), lax.axis_index("gy"), lax.axis_index("gz")
     xs = (lax.rem(ix + nx - 1, nx), lax.rem(ix + 1, nx))
     ys = (lax.rem(iy + ny - 1, ny), lax.rem(iy + 1, ny))
     flip = (1 - 2 * iz).astype(jnp.float32)
+    half = 0.5 * flip
     inner = pl.ds(PAD, ni)
-
-    fields = (
-        (press_in, p0.at[:, inner, :]), (north_in, north), (east_in, up.at[:, inner, :]),
-        (vert_in, head), (geo_in, geo))
-    mass_load = pltpu.make_async_copy(mass_in, mass, load_sem.at[5])
-    mass_load.start()
-    for e, (src, dst) in enumerate(fields):
-        @pl.loop(0, n)
-        def _(m, e=e, src=src, dst=dst):
-            k = iz * (n - 1) + (1 - 2 * iz) * m
-            pltpu.make_async_copy(src.at[k], dst.at[m], load_sem.at[e]).start()
-
-    def loaded(e):
-        pltpu.make_async_copy(fields[e][0], fields[e][1], load_sem.at[e]).wait()
 
     barrier = pltpu.get_barrier_semaphore()
     for t in range(2):
@@ -453,6 +443,24 @@
         pl.semaphore_signal(barrier, inc=1, device_id={"gy": ys[t]})
     pl.semaphore_signal(barrier, inc=1, device_id={"gz": 1 - iz})
 
+    mass_load = pltpu.make_async_copy(mass_in, mass, load_sem.at[5])
+    mass_load.start()
+    fields = (
+        (press_in, p0.at[:, inner, :]), (north_in, north), (east_in, up.at[:, inner, :]),
+        (vert_in, head), (geo_in, geo))
+
+    def load(e, m):
+        src, dst = fields[e]
+        k = iz * (n - 1) + (1 - 2 * iz) * m
+        pltpu.make_async_copy(src.at[k], dst.at[m], load_sem.at[e]).start()
+
+    def loaded(e):
+        pltpu.make_async_copy(fields[e][0], fields[e][1], load_sem.at[e]).wait()
+
+    @pl.loop(0, n)
+    def _(m):
+        load(0, m)
+
     def row_copy(it, t):
         return pltpu.make_async_remote_copy(
             src_ref=row_out.at[it, t], dst_ref=row_in.at[it, 1 - t],
@@ -460,7 +468,7 @@
             device_id={"gx": xs[t]})
 
     def rows_of(s):
-        return pl.ds(pl.multiple_of(s * ROWS, ROWS), ROWS)
+        return pl.ds(pl.multiple_of(s * TILE, TILE), TILE)
 
     def col_copy(it, t, s):
         return pltpu.make_async_remote_copy(
@@ -474,120 +482,135 @@
             send_sem=z_send.at[it, s], recv_sem=z_recv.at[it, s],
             device_id={"gz": 1 - iz})
 
-    lane = lax.broadcasted_iota(jnp.int32, (ROWS, nj), 1)
-    quad, part = lane // 4, lane % 4
-    zero = jnp.zeros((ROWS, nj), jnp.float32)
-
-    def packed(value, m, packs):
-        turned = roll(value, 4 * (m % per) + 2)
+    lane = lax.broadcasted_iota(jnp.int32, (TILE, nj), 1)
+    part, couple, quad = lane % 4, lane // 2, lane // 4
+    zero = jnp.zeros((TILE, nj), jnp.float32)
+    whole = lax.broadcasted_iota(jnp.int32, (ni, nj), 1) % 4
+
+    def placed(mask, value, m, packs):
         b = m // per
-        return tuple(jnp.where(quad == m % per, turned, packs[c]) if c == b else packs[c] for c in range(2))
-
-    def outgoing(it, rows, packs):
+        return tuple(jnp.where(mask, value, packs[c]) if c == b else packs[c] for c in range(2))
+
+    def outgoing(it, rows, part, packs):
         a, b = packs
         col_out[it, 0, rows, :] = jnp.where(part >= 2, a, roll(b, -2))
         col_out[it, 1, rows, :] = jnp.where(part < 2, a, roll(b, 2))
 
-    def incoming(left, right):
-        return (jnp.where(part < 2, roll(right, -2), roll(left, 2)),
-                jnp.where(part < 2, right, left))
-
-    def sides(value, ends, m, width):
-        end = roll(ends[m // per], nj - 2 - 4 * (m % per))
-        low = jnp.where(lane < width, end, roll(value, width))
-        high = jnp.where(lane >= nj - width, end, roll(value, nj - width))
-        return low, high
+    mass_load.wait()
+    inverse = 1.0 / (STIFF * mass[...])
+    con[0] = 1.25 * inverse
+    con[1] = 0.25 * inverse
+    base = 2.0 + inverse
+
+    def pivot(m, a):
+        load(1, m)
+        a = 1.0 / (base - a)
+        coef[m] = a
+        return a
+
+    last = lax.fori_loop(0, n, pivot, jnp.zeros((ni, nj), jnp.float32))
+    con[2] = last / (1.0 - last * last)
+
+    wide = lax.broadcasted_iota(jnp.int32, (WIDE, nj), 1)
+    blank = jnp.zeros((WIDE, nj), jnp.float32)
+    share = n * WIDE // ni
 
     loaded(0)
+
+    @pl.loop(0, ni // WIDE)
+    def _(b):
+        r0 = pl.multiple_of(b * WIDE, WIDE)
+        rows = pl.ds(r0, WIDE)
+        packs = (blank, blank)
+        for m in range(n):
+            value = roll(p0[m, pl.ds(PAD + r0, WIDE), :], 4 * (m % per) + 2)
+            turned_a[m, rows, :] = value
+            packs = placed(wide // 4 == m % per, value, m, packs)
+            if m < share:
+                load(2, b * share + m)
+        packs_p[0, rows, :], packs_p[1, rows, :] = packs
+
     loaded(1)
 
+    @pl.loop(0, ni // WIDE)
+    def _(b):
+        r0 = pl.multiple_of(b * WIDE, WIDE)
+        rows = pl.ds(r0, WIDE)
+        packs = (blank, blank)
+        for m in range(n):
+            q = 4 * (m % per)
+            value = roll(4.0 * north[m, rows, :], q + 1)
+            turned_b[m, rows, :] = turned_a[m, rows, :] + value
+            packs = placed(wide // 2 == q // 2, value, m, packs)
+            if m < share:
+                load(3, b * share + m)
+                load(4, b * share + m)
+        packs_v[0, rows, :], packs_v[1, rows, :] = packs
+
+    edges = []
+    for c in range(2):
+        v = packs_v[c]
+        back = roll(v, 2)
+        edges.append(packs_p[c] + jnp.where(whole == 0, v, jnp.where(whole == 3, -back, 0.0)))
+        packs_v[c] = jnp.where(whole == 1, v, jnp.where(whole == 2, -back, 0.0))
+    outgoing(0, slice(None), whole, edges)
+
+    pl.semaphore_wait(barrier, 5)
+
     @pl.loop(0, count)
-    def _(s):
-        rows = rows_of(s)
-        at = pl.ds(PAD + pl.multiple_of(s * ROWS, ROWS), ROWS)
-        pk, vk = (zero, zero), (zero, zero)
-        for m in range(n):
-            pk = packed(p0[m, at, :], m, pk)
-            vk = packed(north[m, rows, :], m, vk)
-        packs = tuple(
-            a + jnp.where(part == 0, 4.0 * roll(v, -1), jnp.where(part == 3, -4.0 * roll(v, 1), 0.0))
-            for a, v in zip(pk, vk))
-        outgoing(0, rows, packs)
+    def _(t):
+        s = lax.rem(t + 1, count)
+        for t in range(2):
+            col_copy(0, t, s).start()
 
     loaded(2)
     up[:, :PAD, :] = jnp.zeros((n, PAD, nj), jnp.float32)
     up[:, PAD + ni :, :] = jnp.zeros((n, PAD, nj), jnp.float32)
     row_out[0, 0] = p0[:, PAD : PAD + 2, :] - 4.0 * up[:, PAD - 1 : PAD + 1, :]
     row_out[0, 1] = p0[:, PAD + ni - 2 : PAD + ni, :] + 4.0 * up[:, PAD + ni - 1 : PAD + ni + 1, :]
-
-    pl.semaphore_wait(barrier, 5)
-
-    @pl.loop(0, count)
-    def _(s):
-        for t in range(2):
-            col_copy(0, t, s).start()
-
     for t in range(2):
         row_copy(0, t).start()
 
-    mass_load.wait()
-    inverse = 1.0 / (STIFF * mass[...])
-    con[0] = 1.25 * inverse
-    con[1] = 0.25 * inverse
-    base = 2.0 + inverse
-
-    def pivot(m, a):
-        a = 1.0 / (base - a)
-        coef[m] = a
-        return a
-
-    last = lax.fori_loop(0, n, pivot, jnp.zeros((ni, nj), jnp.float32))
-    con[2] = last / (1.0 - last * last)
-
-    @pl.loop(0, count)
-    def _(s):
-        rows = rows_of(s)
-        r0 = PAD + pl.multiple_of(s * ROWS, ROWS)
-        strong = 0.2 * mass[rows, :]
+    @pl.loop(0, ni // WIDE)
+    def _(b):
+        rows = pl.ds(pl.multiple_of(b * WIDE, WIDE), WIDE)
         for m in range(n):
-            v = north[m, rows, :]
-            low = jnp.where(lane < 1, 0.0, roll(v, 1))
-            high = jnp.where(lane >= nj - 1, 0.0, roll(v, nj - 1))
-            dvg[m, rows, :] = strong * (
-                (up[m, pl.ds(r0 + 1, ROWS), :] - up[m, pl.ds(r0 - 1, ROWS), :]) + (high - low))
+            turned_a[m, rows, :] = turned_a[m, rows, :] - roll(4.0 * north[m, rows, :], 4 * (m % per) + 3)
 
     loaded(3)
     loaded(4)
 
-    @pl.loop(0, count)
-    def _(s):
-        rows = rows_of(s)
-        for m in range(n):
-            g = (0.5 * flip) * geo[m, rows, :]
-            geo[m, rows, :] = g
-            head[m, rows, :] = flip * head[m, rows, :] + g
-
     def lateral(it, s):
         rows = rows_of(s)
-        at = pl.ds(PAD + pl.multiple_of(s * ROWS, ROWS), ROWS)
-        ends = incoming(col_in[it, 0, rows, :], col_in[it, 1, rows, :])
+        left, right = col_in[it, 0, rows, :], col_in[it, 1, rows, :]
+        ends = (jnp.where(part < 2, left, right), jnp.where(part < 2, roll(left, -2), roll(right, 2)))
+        if it == 0:
+            ends = [ends[c] + packs_v[c, rows, :] for c in range(2)]
 
         def level(m):
-            low, high = sides(press[it][m, at, :], ends, m, 2)
+            q, end = m % per, ends[m // per]
+            lower = upper = turned[it][m, rows, :]
+            if it == 0:
+                lower = turned_b[m, rows, :]
+            low = roll(jnp.where(couple == 2 * q, end, lower), -4 * q)
+            high = roll(jnp.where(couple == 2 * q + 1, end, upper), -4 * q - 4)
             side[m] = low + high
 
         return level
 
     def forward(it, s):
         rows = rows_of(s)
-        r0 = PAD + pl.multiple_of(s * ROWS, ROWS)
-        at = pl.ds(r0, ROWS)
+        r0 = PAD + pl.multiple_of(s * TILE, TILE)
+        at = pl.ds(r0, TILE)
         weak = 0.05 * mass[rows, :]
         four = 4.0 * weak
         state = {"older": zero, "newer": None, "g": None}
 
         def close(m, above):
-            g = head[m, rows, :] - (above - state["older"])
+            own = head[m, rows, :]
+            if it == 0:
+                own = flip * own + half * geo[m, rows, :]
+            g = own - (above - state["older"])
             if m > 0:
                 g = g + coef[m - 1, rows, :] * state["g"]
             rhs[m, rows, :] = g
@@ -596,8 +619,13 @@
         def level(m):
             ref = press[it]
             p = ref[m, at, :]
-            total = (ref[m, pl.ds(r0 + 2, ROWS), :] + ref[m, pl.ds(r0 - 2, ROWS), :]) + side[m]
-            d = (dvg[m, rows, :] + four * p) - weak * total
+            total = (ref[m, pl.ds(r0 + 2, TILE), :] + ref[m, pl.ds(r0 - 2, TILE), :]) + side[m]
+            d = four * p
+            if it == 0:
+                total = total - 4.0 * (up[m, pl.ds(r0 + 1, TILE), :] - up[m, pl.ds(r0 - 1, TILE), :])
+            else:
+                d = dvg[m, rows, :] + d
+            d = d - weak * total
             if it < ITERS - 1:
                 dvg[m, rows, :] = d
             else:
@@ -627,99 +655,126 @@
         press[it][:, PAD - 2 : PAD, :] = row_in[it, 0]
         press[it][:, PAD + ni : PAD + ni + 2, :] = row_in[it, 1]
 
-    def pass_one(it):
-        col_wait(it, 1)
-        level = lateral(it, 1)
-        for m in range(n):
-            level(m)
-
-        @pl.loop(1, count)
-        def _(s):
-            @pl.when(s == count - 1)
-            def _():
-                row_wait(it)
-
-            after = lax.rem(s + 1, count)
-            col_wait(it, after)
-            level, finish = forward(it, s)
-            ahead = lateral(it, after)
-            for m in range(n):
-                level(m)
-                ahead(m)
-            finish()
-
-        level, finish = forward(it, 0)
-        for m in range(n):
-            level(m)
-        finish()
-
-    def interface(it, s):
-        rows = rows_of(s)
-        z_copy(it, s).wait()
-        a, w = coef[n - 1, rows, :], con[2, rows, :]
-        mine = z_out[it, 0, rows, :] - z_in[it, 1, rows, :]
-        other = z_in[it, 0, rows, :] - z_out[it, 1, rows, :]
+    def meet(a, w, out, inn):
+        mine, other = out[0] - inn[1], inn[0] - out[1]
         z = w * (mine - a * other)
         return z, a * (z - other)
 
     def backward(it, s):
         rows = rows_of(s)
-        at = pl.ds(PAD + pl.multiple_of(s * ROWS, ROWS), ROWS)
+        at = pl.ds(PAD + pl.multiple_of(s * TILE, TILE), TILE)
         near, far = con[0, rows, :], con[1, rows, :]
-        z, above = interface(it, s)
-        packs = (zero, zero)
-        for m in range(n - 1, -1, -1):
+        z_copy(it, s).wait()
+        state = {"packs": (zero, zero)}
+        state["z"], state["above"] = meet(
+            coef[n - 1, rows, :], con[2, rows, :],
+            [z_out[it, c, rows, :] for c in range(2)], [z_in[it, c, rows, :] for c in range(2)])
+
+        def level(m):
+            z = state["z"]
             g = geo[m, rows, :]
+            if it == 0:
+                g = half * g
             head[m, rows, :] = near * z + g
             geo[m, rows, :] = far * z + g
             below = coef[m - 1, rows, :] * (rhs[m - 1, rows, :] + z) if m > 0 else zero
-            p = star[m, rows, :] - (0.5 / STIFF) * (above - below)
+            p = star[m, rows, :] - (0.5 / STIFF) * (state["above"] - below)
             press[it + 1][m, at, :] = p
-            packs = packed(p, m, packs)
-            above, z = z, below
-        outgoing(it + 1, rows, packs)
-        for t in range(2):
-            col_copy(it + 1, t, s).start()
-
-    def pass_two(it):
-        @pl.loop(0, count)
-        def _(t):
-            s = jnp.where(t < FRONT, t + 1, jnp.where(t == FRONT, count - 1, jnp.where(t == FRONT + 1, 0, t - 1)))
-            backward(it, s)
-
-            @pl.when(t == FRONT)
+            value = roll(p, 4 * (m % per) + 2)
+            turned[it + 1][m, rows, :] = value
+            state["packs"] = placed(quad == m % per, value, m, state["packs"])
+            state["above"], state["z"] = z, below
+
+        def finish():
+            outgoing(it + 1, rows, part, state["packs"])
+            for t in range(2):
+                col_copy(it + 1, t, s).start()
+
+        return level, finish
+
+    for it in range(ITERS):
+        final = it == ITERS - 1
+        front = (count - 2, count - 2, count - 2)[it]
+        lag = count if final else LAG
+
+        def order(t, front=front):
+            return jnp.where(t < front, t + 1, jnp.where(t == front, count - 1, jnp.where(t == front + 1, 0, t - 1)))
+
+        def ahead_of(t, it=it, front=front, order=order):
+            @pl.when(t == front)
+            def _():
+                row_wait(it)
+
+            after = order(lax.rem(t + 1, count))
+
+            @pl.when(t < count - 1)
+            def _():
+                col_wait(it, after)
+
+            return forward(it, order(t)) + (lateral(it, after),)
+
+        def behind(u, it=it, order=order):
+            return backward(it, order(u))
+
+        def send_rows(u, it=it, front=front):
+            @pl.when(u == front)
             def _():
                 row_out[it + 1, 1] = press[it + 1][:, PAD + ni - 2 : PAD + ni, :]
                 row_copy(it + 1, 1).start()
 
-            @pl.when(t == FRONT + 1)
+            @pl.when(u == front + 1)
             def _():
                 row_out[it + 1, 0] = press[it + 1][:, PAD : PAD + 2, :]
                 row_copy(it + 1, 0).start()
 
-    for it in range(ITERS):
-        pass_one(it)
-        if it < ITERS - 1:
-            pass_two(it)
+        col_wait(it, order(0))
+        first = lateral(it, order(0))
+        for m in range(n):
+            first(m)
+
+        @pl.loop(0, lag)
+        def _(t):
+            one, finish, ahead = ahead_of(t)
+            for m in range(n):
+                one(m)
+                ahead(m)
+            finish()
+
+        if not final:
+            @pl.loop(lag, count)
+            def _(t):
+                one, finish, ahead = ahead_of(t)
+                for m in range(n):
+                    one(m)
+                    ahead(m)
+                finish()
+                two, deliver = behind(t - lag)
+                for m in range(n):
+                    two(n - 1 - m)
+                deliver()
+                send_rows(t - lag)
+
+            @pl.loop(count - lag, count)
+            def _(u):
+                two, deliver = behind(u)
+                for m in range(n):
+                    two(n - 1 - m)
+                deliver()
+                send_rows(u)
 
     for t, at in ((0, PAD - 2), (1, PAD + ni)):
         p0[:, at : at + 2, :] = (row_in[0, t] + row_in[1, t]) + row_in[2, t]
-
-    def closing(s):
-        rows = rows_of(s)
-        left = (col_in[0, 0, rows, :] + col_in[1, 0, rows, :]) + col_in[2, 0, rows, :]
-        right = (col_in[0, 1, rows, :] + col_in[1, 1, rows, :]) + col_in[2, 1, rows, :]
-        edge[0, rows, :] = jnp.where(part == 1, roll(right, -1), roll(left, 1))
-        edge[1, rows, :] = jnp.where(part == 1, roll(right, 1), roll(left, -1))
+    left = (col_in[0, 0] + col_in[1, 0]) + col_in[2, 0]
+    right = (col_in[0, 1] + col_in[1, 1]) + col_in[2, 1]
+    edge[0] = jnp.where(whole == 1, roll(right, -1), roll(left, 1))
+    edge[1] = jnp.where(whole == 1, roll(right, 1), roll(left, -1))
 
     @pl.loop(0, count)
     def _(s):
-        closing(s)
-
-    @pl.loop(0, count)
-    def _(t):
-        s = lax.rem(t + 1, count)
-        faces[0, rows_of(s), :], faces[1, rows_of(s), :] = interface(ITERS - 1, s)
+        z_copy(ITERS - 1, s).wait()
+
+    faces[0], faces[1] = meet(
+        coef[n - 1], con[2], [z_out[ITERS - 1, c] for c in range(2)], [z_in[ITERS - 1, c] for c in range(2)])
 
 
 def finale(n, ni, nj, rhs, star, geo, coef, psum, up, north, edge, faces, mass,
@@ -780,7 +835,7 @@
 def pair(sizes, east, north, vert, geo, press, mass):
     n, ni, nj = east.shape
     f32 = jnp.float32
-    count = ni // ROWS
+    count = ni // TILE
     shape = (n, ni, nj)
     padded = (n, ni + 2 * PAD, nj)
     kept = [shape, shape, shape, shape, padded, padded, shape, (2, ni, nj), (2, ni, nj)]
@@ -788,13 +843,15 @@
     state = pl.pallas_call(
         functools.partial(paired, n, ni, nj, sizes),
         out_shape=[pltpu.VMEM(s, f32) for s in kept],
-        in_specs=[pl.BlockSpec(memory_space=pl.ANY)] * 6,
+        in_specs=[pl.BlockSpec(memory_space=pltpu.HBM)] * 6,
         out_specs=[vmem] * len(kept),
         scratch_shapes=[
             pltpu.VMEM(padded, f32), pltpu.VMEM(padded, f32), pltpu.VMEM(shape, f32), pltpu.VMEM(shape, f32),
-            pltpu.VMEM((n, ROWS, nj), f32),
+            pltpu.VMEM(shape, f32), pltpu.VMEM(shape, f32), pltpu.VMEM(shape, f32),
+            pltpu.VMEM((n, TILE, nj), f32),
             pltpu.VMEM((ni, nj), f32),
             pltpu.VMEM((3, ni, nj), f32),
+            pltpu.VMEM((2, ni, nj), f32),
             pltpu.VMEM((2, ni, nj), f32),
             pltpu.VMEM((ITERS, 2, n, 2, nj), f32),
             pltpu.VMEM((ITERS, 2, n, 2, nj), f32),
@@ -811,7 +868,7 @@
             pltpu.SemaphoreType.DMA((ITERS, count)),
         ],
         compiler_params=pltpu.CompilerParams(
-            collective_id=0, has_side_effects=True, vmem_limit_bytes=25 * 1024 * 1024),
+            collective_id=0, has_side_effects=True, vmem_limit_bytes=41 * 1024 * 1024),
     )(east, north, vert, geo, press, mass)
     return pl.pallas_call(
         functools.partial(finale, n, ni, nj),
@@ -829,7 +886,7 @@
 
     def body(east, *rest):
         n, ni, nj = east.shape
-        fits = sizes[2] == 2 and n <= nj // 2 and ni // ROWS > FRONT + 2 and ITERS == 3
+        fits = sizes[2] == 2 and n <= nj // 2 and ni % TILE == 0 and ni // TILE > LAG and ni % WIDE == 0 and n * WIDE % ni == 0 and ITERS == 3
         return (pair if fits else local)(sizes, east, *rest)
 
     return jax.shard_map(

time: 51.8 us -> 36.3 us (0.70)
  Pallas kernels: 46.3 us -> 35.5 us
  local copies, waits for them, and re-layouts: 4.61 us -> 0.01 us
    pallas_call x1, Pallas kernels: 40.4 us -> 29.5 us  [pair(): pl.pallas_call(functools.partial(paired, n, ni, nj, sizes), out_shape=[pl...]
    unnamed x6 -> x2, local copies, waits for them, and re-layouts: 4.61 us -> 0.01 us
where the time goes in v2:
time: 36.3 us; the launch traced here: 36.1 us
  Pallas kernels  35.5 us (98%)
  between operations  0.66 us (2%)
    pallas_call x1, Pallas kernels, pair(): pl.pallas_call(functools.partial(paired, n, ni, nj, sizes), out_shape=[pl...  29.5 us
    pallas_call x1, Pallas kernels, pair(): pl.pallas_call(functools.partial(finale, n, ni, nj), out_shape=[jax.Shape...  5.94 us

profile of v2, /device:TPU:0, one launch (start us, length us, event | category | flops | bytes accessed | tf_op | source)
XLA Modules:
  0.0 36.1 jit_solution(14832602883531420516)
XLA Ops:
  0.6 0.0 copy-start
  0.6 29.5 %shard_map.101 = (f32[48,128,128]{2,1,0:T(8,128)S(1)}, f32[48,128,128]{2,1,0:T(8,128)S(1)}, f32[48,128,128]{2,1,0:T(8,128)S(1)}, f32[48,128,128]{2,1,0:T(8,128)S...) custom-call(f32[48,128,128]{2,1,0:T(8,128)} %east_in.1, ...), custom_call_target="tpu_custom_call" | custom-call | tf_op jit(solution)/shard_map/pallas_call | solution.py:843
  30.2 0.0 copy-done
  30.2 5.9 %shard_map.102 = (f32[48,128,128]{2,1,0:T(8,128)}, f32[48,128,128]{2,1,0:T(8,128)}, f32[48,128,128]{2,1,0:T(8,128)}, f32[48,128,128]{2,1,0:T(8,128)}, f32[48,128,128]{2,1,0:T(8,128)}) custom-call(f32[48,128,128]{2,1,0:T(8,128)S(1)} %get-tuple-element.14.rhs, f32[48,128,128]{2,1,0:T(8,128)S(1)} %get-tuple-element.15.star, ...), custom_call_target="tpu_custom_call" | custom-call | tf_op jit(solution)/shard_map/pallas_call | solution.py:873
Async XLA Ops:
  0.6 29.6 %copy-start = (f32[128,128]{1,0:T(8,128)S(1)}, f32[128,128]{1,0:T(8,128)}, u32[]{:S(2)}) copy-start(f32[128,128]{1,0:T(8,128)} %mass.1) | copy-start | bytes 196612

commit v3 on v2

--- a/solution.py
+++ b/solution.py
@@ -415,8 +415,8 @@
     )(east, north, vert, geo, press, mass)
 
 
-LAG = 3
-TILE = 32
+LAG = 5
+TILE = 16
 WIDE = 32
 
 
@@ -424,7 +424,7 @@
            rhs, star, geo, coef, p0, up, north, edge, faces,
            p1, p2, dvg, head, turned_a, turned_b, turned_c, side, mass, con, packs_p, packs_v,
            row_out, row_in, col_out, col_in, z_out, z_in,
-           load_sem, row_send, row_recv, col_send, col_recv, z_send, z_recv):
+           load_sem, sent, row_recv, col_recv, z_recv):
     nx, ny, _ = sizes
     per = nj // 4
     count = ni // TILE
@@ -464,8 +464,13 @@
     def row_copy(it, t):
         return pltpu.make_async_remote_copy(
             src_ref=row_out.at[it, t], dst_ref=row_in.at[it, 1 - t],
-            send_sem=row_send.at[it, t], recv_sem=row_recv.at[it, 1 - t],
+            send_sem=sent.at[0], recv_sem=row_recv.at[it],
             device_id={"gx": xs[t]})
+
+    def arrived(out, inn, e, sem, axis):
+        pltpu.make_async_remote_copy(
+            src_ref=out, dst_ref=inn, send_sem=sent.at[e], recv_sem=sem,
+            device_id={axis: 1 - iz if axis == "gz" else xs[0] if axis == "gx" else ys[0]}).wait_recv()
 
     def rows_of(s):
         return pl.ds(pl.multiple_of(s * TILE, TILE), TILE)
@@ -473,13 +478,13 @@
     def col_copy(it, t, s):
         return pltpu.make_async_remote_copy(
             src_ref=col_out.at[it, t, rows_of(s), :], dst_ref=col_in.at[it, 1 - t, rows_of(s), :],
-            send_sem=col_send.at[it, t, s], recv_sem=col_recv.at[it, 1 - t, s],
+            send_sem=sent.at[1], recv_sem=col_recv.at[it, s],
             device_id={"gy": ys[t]})
 
     def z_copy(it, s):
         return pltpu.make_async_remote_copy(
             src_ref=z_out.at[it, :, rows_of(s), :], dst_ref=z_in.at[it, :, rows_of(s), :],
-            send_sem=z_send.at[it, s], recv_sem=z_recv.at[it, s],
+            send_sem=sent.at[2], recv_sem=z_recv.at[it, s],
             device_id={"gz": 1 - iz})
 
     lane = lax.broadcasted_iota(jnp.int32, (TILE, nj), 1)
@@ -646,12 +651,10 @@
         return level, finish
 
     def col_wait(it, s):
-        for t in range(2):
-            col_copy(it, t, s).wait()
+        arrived(col_out.at[it, :, rows_of(s), :], col_in.at[it, :, rows_of(s), :], 1, col_recv.at[it, s], "gy")
 
     def row_wait(it):
-        for t in range(2):
-            row_copy(it, t).wait()
+        arrived(row_out.at[it], row_in.at[it], 0, row_recv.at[it], "gx")
         press[it][:, PAD - 2 : PAD, :] = row_in[it, 0]
         press[it][:, PAD + ni : PAD + ni + 2, :] = row_in[it, 1]
 
@@ -664,7 +667,7 @@
         rows = rows_of(s)
         at = pl.ds(PAD + pl.multiple_of(s * TILE, TILE), TILE)
         near, far = con[0, rows, :], con[1, rows, :]
-        z_copy(it, s).wait()
+        z_copy(it, s).wait_recv()
         state = {"packs": (zero, zero)}
         state["z"], state["above"] = meet(
             coef[n - 1, rows, :], con[2, rows, :],
@@ -771,20 +774,25 @@
 
     @pl.loop(0, count)
     def _(s):
-        z_copy(ITERS - 1, s).wait()
+        z_copy(ITERS - 1, s).wait_recv()
 
     faces[0], faces[1] = meet(
         coef[n - 1], con[2], [z_out[ITERS - 1, c] for c in range(2)], [z_in[ITERS - 1, c] for c in range(2)])
+
+    for e, out, inn, axis in ((0, row_out, row_in, "gx"), (1, col_out, col_in, "gy"), (2, z_out, z_in, "gz")):
+        pltpu.make_async_remote_copy(
+            src_ref=out, dst_ref=inn, send_sem=sent.at[e], recv_sem=load_sem.at[e],
+            device_id={axis: 1 - iz if axis == "gz" else xs[0] if axis == "gx" else ys[0]}).wait_send()
 
 
 def finale(n, ni, nj, rhs, star, geo, coef, psum, up, north, edge, faces, mass,
            east_out, north_out, vert_out, geo_out, press_out,
            east_s, north_s, vert_s, geo_s, press_s, sem):
     per = nj // 4
-    count = ni // ROWS
+    count = ni // WIDE
     iz = lax.axis_index("gz")
     flip = (1 - 2 * iz).astype(jnp.float32)
-    lane = lax.broadcasted_iota(jnp.int32, (ROWS, nj), 1)
+    lane = lax.broadcasted_iota(jnp.int32, (WIDE, nj), 1)
 
     def store(e, src, dst, rows):
         return pltpu.make_async_copy(src.at[:, rows, :], dst.at[:, rows, :], sem.at[e])
@@ -796,7 +804,7 @@
 
     @pl.loop(0, count)
     def _(s):
-        rows = pl.ds(pl.multiple_of(s * ROWS, ROWS), ROWS)
+        rows = pl.ds(pl.multiple_of(s * WIDE, WIDE), WIDE)
         v_of = flip / (STIFF * mass[rows, :])
         half = 0.5 * v_of
         twice = 2.0 * flip
@@ -813,18 +821,18 @@
 
     @pl.loop(0, count)
     def _(s):
-        rows = pl.ds(pl.multiple_of(s * ROWS, ROWS), ROWS)
-        r0 = PAD + pl.multiple_of(s * ROWS, ROWS)
+        rows = pl.ds(pl.multiple_of(s * WIDE, WIDE), WIDE)
+        r0 = PAD + pl.multiple_of(s * WIDE, WIDE)
         ends = (edge[0, rows, :], edge[1, rows, :])
         for m in range(n):
             k = level_of(m)
-            p = psum[m, pl.ds(r0, ROWS), :]
+            p = psum[m, pl.ds(r0, WIDE), :]
             end = roll(ends[m // per], nj - 2 - 4 * (m % per))
             low = jnp.where(lane < 1, end, roll(p, 1))
             high = jnp.where(lane >= nj - 1, end, roll(p, nj - 1))
             north_s[k, rows, :] = north[m, rows, :] - 0.25 * (high - low)
-            east_s[k, rows, :] = up[m, pl.ds(r0, ROWS), :] - 0.25 * (
-                psum[m, pl.ds(r0 + 1, ROWS), :] - psum[m, pl.ds(r0 - 1, ROWS), :])
+            east_s[k, rows, :] = up[m, pl.ds(r0, WIDE), :] - 0.25 * (
+                psum[m, pl.ds(r0 + 1, WIDE), :] - psum[m, pl.ds(r0 - 1, WIDE), :])
         for e in (0, 1):
             store(e, *outs[e], rows).start()
 
@@ -860,10 +868,8 @@
             pltpu.VMEM((ITERS, 2, ni, nj), f32),
             pltpu.VMEM((ITERS, 2, ni, nj), f32),
             pltpu.SemaphoreType.DMA((6,)),
-            pltpu.SemaphoreType.DMA((ITERS, 2)),
-            pltpu.SemaphoreType.DMA((ITERS, 2)),
-            pltpu.SemaphoreType.DMA((ITERS, 2, count)),
-            pltpu.SemaphoreType.DMA((ITERS, 2, count)),
+            pltpu.SemaphoreType.DMA((3,)),
+            pltpu.SemaphoreType.DMA((ITERS,)),
             pltpu.SemaphoreType.DMA((ITERS, count)),
             pltpu.SemaphoreType.DMA((ITERS, count)),
         ],

time: 36.3 us -> 35.3 us (0.972)
  Pallas kernels: 35.5 us -> 34.5 us
    pallas_call x1, Pallas kernels: 29.5 us -> 28.5 us  [pair(): pl.pallas_call(functools.partial(paired, n, ni, nj, sizes), out_shape=[pl...]
where the time goes in v3:
time: 35.3 us; the launch traced here: 35.2 us
  Pallas kernels  34.5 us (98%)
  between operations  0.66 us (2%)
    pallas_call x1, Pallas kernels, pair(): pl.pallas_call(functools.partial(paired, n, ni, nj, sizes), out_shape=[pl...  28.5 us
    pallas_call x1, Pallas kernels, pair(): pl.pallas_call(functools.partial(finale, n, ni, nj), out_shape=[jax.Shape...  5.99 us

profile of v3, /device:TPU:0, one launch (start us, length us, event | category | flops | bytes accessed | tf_op | source)
XLA Modules:
  0.0 35.2 jit_solution(501739321278319791)
XLA Ops:
  0.6 0.0 copy-start
  0.6 28.5 %shard_map.101 = (f32[48,128,128]{2,1,0:T(8,128)S(1)}, f32[48,128,128]{2,1,0:T(8,128)S(1)}, f32[48,128,128]{2,1,0:T(8,128)S(1)}, f32[48,128,128]{2,1,0:T(8,128)S...) custom-call(f32[48,128,128]{2,1,0:T(8,128)} %east_in.1, ...), custom_call_target="tpu_custom_call" | custom-call | tf_op jit(solution)/shard_map/pallas_call | solution.py:851
  29.2 0.0 copy-done
  29.2 6.0 %shard_map.102 = (f32[48,128,128]{2,1,0:T(8,128)}, f32[48,128,128]{2,1,0:T(8,128)}, f32[48,128,128]{2,1,0:T(8,128)}, f32[48,128,128]{2,1,0:T(8,128)}, f32[48,128,128]{2,1,0:T(8,128)}) custom-call(f32[48,128,128]{2,1,0:T(8,128)S(1)} %get-tuple-element.14.rhs, f32[48,128,128]{2,1,0:T(8,128)S(1)} %get-tuple-element.15.star, ...), custom_call_target="tpu_custom_call" | custom-call | tf_op jit(solution)/shard_map/pallas_call | solution.py:879
Async XLA Ops:
  0.6 28.5 %copy-start = (f32[128,128]{1,0:T(8,128)S(1)}, f32[128,128]{1,0:T(8,128)}, u32[]{:S(2)}) copy-start(f32[128,128]{1,0:T(8,128)} %mass.1) | copy-start | bytes 196612

commit v4 on v3

--- a/solution.py
+++ b/solution.py
@@ -478,13 +478,13 @@
     def col_copy(it, t, s):
         return pltpu.make_async_remote_copy(
             src_ref=col_out.at[it, t, rows_of(s), :], dst_ref=col_in.at[it, 1 - t, rows_of(s), :],
-            send_sem=sent.at[1], recv_sem=col_recv.at[it, s],
+            send_sem=sent.at[1], recv_sem=col_recv.at[it % 2, s],
             device_id={"gy": ys[t]})
 
     def z_copy(it, s):
         return pltpu.make_async_remote_copy(
             src_ref=z_out.at[it, :, rows_of(s), :], dst_ref=z_in.at[it, :, rows_of(s), :],
-            send_sem=sent.at[2], recv_sem=z_recv.at[it, s],
+            send_sem=sent.at[2], recv_sem=z_recv.at[it % 2, s],
             device_id={"gz": 1 - iz})
 
     lane = lax.broadcasted_iota(jnp.int32, (TILE, nj), 1)
@@ -651,7 +651,7 @@
         return level, finish
 
     def col_wait(it, s):
-        arrived(col_out.at[it, :, rows_of(s), :], col_in.at[it, :, rows_of(s), :], 1, col_recv.at[it, s], "gy")
+        arrived(col_out.at[it, :, rows_of(s), :], col_in.at[it, :, rows_of(s), :], 1, col_recv.at[it % 2, s], "gy")
 
     def row_wait(it):
         arrived(row_out.at[it], row_in.at[it], 0, row_recv.at[it], "gx")
@@ -870,8 +870,8 @@
             pltpu.SemaphoreType.DMA((6,)),
             pltpu.SemaphoreType.DMA((3,)),
             pltpu.SemaphoreType.DMA((ITERS,)),
-            pltpu.SemaphoreType.DMA((ITERS, count)),
-            pltpu.SemaphoreType.DMA((ITERS, count)),
+            pltpu.SemaphoreType.DMA((2, count)),
+            pltpu.SemaphoreType.DMA((2, count)),
         ],
         compiler_params=pltpu.CompilerParams(
             collective_id=0, has_side_effects=True, vmem_limit_bytes=41 * 1024 * 1024),

time: 35.3 us -> 35.2 us (level)
  no operation moved by 1% of the time
where the time goes in v4:
time: 35.2 us; the launch traced here: 35 us
  Pallas kernels  34.3 us (97%)
  between operations  0.66 us (2%)
    pallas_call x1, Pallas kernels, pair(): pl.pallas_call(functools.partial(paired, n, ni, nj, sizes), out_shape=[pl...  28.4 us
    pallas_call x1, Pallas kernels, pair(): pl.pallas_call(functools.partial(finale, n, ni, nj), out_shape=[jax.Shape...  5.99 us

profile of v4, /device:TPU:0, one launch (start us, length us, event | category | flops | bytes accessed | tf_op | source)
XLA Modules:
  0.0 35.0 jit_solution(6211717339880839367)
XLA Ops:
  0.6 0.0 copy-start
  0.6 28.4 %shard_map.101 = (f32[48,128,128]{2,1,0:T(8,128)S(1)}, f32[48,128,128]{2,1,0:T(8,128)S(1)}, f32[48,128,128]{2,1,0:T(8,128)S(1)}, f32[48,128,128]{2,1,0:T(8,128)S...) custom-call(f32[48,128,128]{2,1,0:T(8,128)} %east_in.1, ...), custom_call_target="tpu_custom_call" | custom-call | tf_op jit(solution)/shard_map/pallas_call | solution.py:851
  29.0 0.0 copy-done
  29.0 6.0 %shard_map.102 = (f32[48,128,128]{2,1,0:T(8,128)}, f32[48,128,128]{2,1,0:T(8,128)}, f32[48,128,128]{2,1,0:T(8,128)}, f32[48,128,128]{2,1,0:T(8,128)}, f32[48,128,128]{2,1,0:T(8,128)}) custom-call(f32[48,128,128]{2,1,0:T(8,128)S(1)} %get-tuple-element.14.rhs, f32[48,128,128]{2,1,0:T(8,128)S(1)} %get-tuple-element.15.star, ...), custom_call_target="tpu_custom_call" | custom-call | tf_op jit(solution)/shard_map/pallas_call | solution.py:879
Async XLA Ops:
  0.6 28.4 %copy-start = (f32[128,128]{1,0:T(8,128)S(1)}, f32[128,128]{1,0:T(8,128)}, u32[]{:S(2)}) copy-start(f32[128,128]{1,0:T(8,128)} %mass.1) | copy-start | bytes 196612
